TPU v7x, 32 devices: a whole 2x2x4 slice. The times are simulated.
32 devices in a mesh: seq: 8 (over z, x), head: 4 (over y, core).
Axes of the slice: x: 2, y: 2, z: 4, core: 2. Of those that a mesh axis runs over, the one named last changes fastest.
Arguments:
- query_in: bfloat16 [2048, 8192], P('seq', 'head'), may hold values from -1.796875 to 1.796875
- key_in: bfloat16 [2048, 8192], P('seq', 'head'), may hold values from -1.796875 to 1.796875
- value_in: bfloat16 [2048, 8192], P('seq', 'head'), may hold values from -11 to 11
- log_decay: float32 [2048, 64], P('seq', 'head'), may hold values from -1 to 0, as said below
- norm_gain: float32 [8192], P('head'), may hold values from 0.5 to 1.5
- prompt_lengths: int32 [4], replicated, may hold values from 1 to 1536, 2048 in all
- step_query: bfloat16 [4, 128, 8192], P(None, 'seq', 'head'), may hold values from -1.796875 to 1.796875
- step_key: bfloat16 [4, 128, 8192], P(None, 'seq', 'head'), may hold values from -1.796875 to 1.796875
- step_value: bfloat16 [4, 128, 8192], P(None, 'seq', 'head'), may hold values from -6 to 6
- step_decay: float32 [4, 128, 64], P(None, 'seq', 'head'), may hold values from -0.3 to -0.01
- row_prompt: int32 [128], P('seq'), may hold values from 0 to 3
Outputs:
- attn_out: bfloat16 [2048, 8192], P('seq', 'head')
- decode_out: bfloat16 [4, 128, 8192], P(None, 'seq', 'head')
Inputs may be any that keep to these rules, and one draw needn't show every extreme that they name: `log_decay`: Negative; per head and token.
All inputs are finite; a program needn't handle non-finite values.
Results may differ from a plain program's by a relative error of at most 0.0056.
Values sent between devices are 32-bit elements; how exact they have to be, the bound alone decides.
A program may use at most 64 MiB of HBM per device.

v0:
```python
import jax
import jax.numpy as jnp
from jax import lax
from jax.sharding import PartitionSpec as P

HEAD_COUNT = 64
HDIM = 128
BLOCK = 256
PROMPTS = 4
EPSILON = 1e-06


def carried_in(part, axis, combine, identity):
    place = lax.axis_index(axis)
    gathered = jax.tree.map(lambda a: lax.all_gather(a, axis), part)
    state = jax.tree.map(lambda a, e: jnp.zeros_like(a) + jnp.asarray(e, a.dtype), part, identity)

    def one(step, state):
        return combine(
            state, jax.tree.map(lambda a: lax.dynamic_index_in_dim(a, step, 0, False), gathered)
        )

    return lax.fori_loop(0, place, one, state)


def segment_ids(prompt_lengths, positions):
    boundary = jnp.cumsum(prompt_lengths)
    return jnp.sum((positions[:, None] >= boundary[None, :]).astype(jnp.int32), axis=1)


def combine_pairs(earlier, later):
    return (earlier[0] * later[0], later[0][:, None, None] * earlier[1] + later[1])


def local(
    query_in,
    key_in,
    value_in,
    log_decay,
    norm_gain,
    prompt_lengths,
    step_query,
    step_key,
    step_value,
    step_decay,
    row_prompt,
):
    tok_count = query_in.shape[0]
    heads_here = log_decay.shape[1]
    nblocks = tok_count // BLOCK
    first = lax.axis_index("seq") * tok_count
    positions = first + jnp.arange(tok_count, dtype=jnp.int32)
    segs = segment_ids(prompt_lengths, positions)
    seg_entry = jnp.where(first > 0, segment_ids(prompt_lengths, (first - 1)[None])[0], -1)
    shape4 = (nblocks, BLOCK, heads_here, HDIM)
    queries = query_in.reshape(shape4)
    keys_blk = key_in.reshape(shape4)
    values_blk = value_in.reshape(shape4)
    cumul = jnp.cumsum(log_decay.reshape(nblocks, BLOCK, heads_here), axis=1)
    seg_blocks = segs.reshape(nblocks, BLOCK)
    seg_front = jnp.concatenate([seg_entry[None], seg_blocks[:-1, -1]])
    causal = jnp.arange(BLOCK)[:, None] >= jnp.arange(BLOCK)[None, :]
    linked = (causal[None] & (seg_blocks[:, :, None] == seg_blocks[:, None, :]))[:, None]
    cum_heads = jnp.transpose(cumul, (0, 2, 1))
    spread = cum_heads[:, :, :, None] - cum_heads[:, :, None, :]
    factor = jnp.where(linked, jnp.exp(jnp.where(linked, spread, 0.0)), 0.0)
    scores = jnp.einsum("nthd,nshd->nhts", queries, keys_blk, preferred_element_type=jnp.float32)
    weights = (scores * factor).astype(jnp.bfloat16)
    inner = jnp.einsum("nhts,nshd->nthd", weights, values_blk, preferred_element_type=jnp.float32)
    keep = (
        jnp.exp(cumul[:, -1:, :] - cumul)
        * (seg_blocks == seg_blocks[:, -1:]).astype(jnp.float32)[:, :, None]
    )
    keyed = (keys_blk.astype(jnp.float32) * keep[..., None]).astype(jnp.bfloat16)
    updates = jnp.einsum("nshd,nshe->nhde", keyed, values_blk, preferred_element_type=jnp.float32)
    onward = (
        jnp.exp(cumul[:, -1, :]) * (seg_blocks[:, -1] == seg_front).astype(jnp.float32)[:, None]
    )
    local_states = [jnp.zeros((heads_here, HDIM, HDIM), jnp.float32)]
    growth = [jnp.ones((heads_here,), jnp.float32)]
    blk_index = 0
    local_states.append(onward[blk_index][:, None, None] * local_states[-1] + updates[blk_index])
    growth.append(onward[blk_index] * growth[-1])
    summary = (growth[-1], local_states[-1])
    identity = (
        jnp.ones((heads_here,), jnp.float32),
        jnp.zeros((heads_here, HDIM, HDIM), jnp.float32),
    )
    entry = carried_in(summary, "seq", combine_pairs, identity)
    entry_state = entry[1]
    start_states = jnp.stack([local_states[0] + growth[0][:, None, None] * entry_state])
    state_half = start_states.astype(jnp.bfloat16)
    carried = jnp.exp(cumul) * (seg_blocks == seg_front[:, None]).astype(jnp.float32)[:, :, None]
    outer = (
        jnp.einsum("nthd,nhde->nthe", queries, state_half, preferred_element_type=jnp.float32)
        * carried[..., None]
    )
    mixed = (inner + outer).reshape(tok_count, heads_here * HDIM)
    squares = lax.psum(jnp.sum(mixed * mixed, axis=1), "head")
    scale = lax.rsqrt(squares / (HEAD_COUNT * HDIM) + EPSILON)
    attn_out = (mixed * scale[:, None] * norm_gain[None, :]).astype(jnp.bfloat16)
    boundary = jnp.cumsum(prompt_lengths)

    def prompt_end(prompt):
        last_tok = boundary[prompt] - 1
        local_tok = last_tok - first
        owned = (local_tok >= 0) & (local_tok < tok_count)
        safe_tok = jnp.clip(local_tok, 0, tok_count - 1)
        blk_index = safe_tok // BLOCK
        offset = safe_tok - blk_index * BLOCK
        cum_blk = cumul[blk_index]
        reached = cum_blk[offset]
        taken = (jnp.arange(BLOCK) <= offset) & (seg_blocks[blk_index] == prompt)
        keep_end = (
            jnp.exp(jnp.where(taken[:, None], reached[None, :] - cum_blk, 0.0))
            * taken.astype(jnp.float32)[:, None]
        )
        tailed = (keys_blk[blk_index].astype(jnp.float32) * keep_end[:, :, None]).astype(
            jnp.bfloat16
        )
        part = jnp.einsum(
            "shd,she->hde", tailed, values_blk[blk_index], preferred_element_type=jnp.float32
        )
        lead = jnp.exp(reached) * (seg_front[blk_index] == prompt).astype(jnp.float32)
        total = lead[:, None, None] * start_states[blk_index] + part
        return total * owned.astype(jnp.float32)

    candidates = lax.map(prompt_end, jnp.arange(PROMPTS, dtype=jnp.int32))
    prompt_state = lax.psum(candidates, "seq")
    rows_here = row_prompt.shape[0]
    row_states = jnp.take(prompt_state, row_prompt, axis=0)
    results = []
    for section in range(step_query.shape[0]):
        query_now = step_query[section].astype(jnp.float32).reshape(rows_here, heads_here, HDIM)
        key_now = step_key[section].astype(jnp.float32).reshape(rows_here, heads_here, HDIM)
        value_now = step_value[section].astype(jnp.float32).reshape(rows_here, heads_here, HDIM)
        row_states = (
            jnp.exp(step_decay[section])[:, :, None, None] * row_states
            + key_now[:, :, :, None] * value_now[:, :, None, :]
        )
        results.append(
            jnp.einsum(
                "rhd,rhde->rhe", query_now, row_states, precision=lax.Precision.HIGHEST
            ).reshape(rows_here, heads_here * HDIM)
        )
    decoded = jnp.stack(results)
    step_squares = lax.psum(jnp.sum(decoded * decoded, axis=2), "head")
    step_scale = lax.rsqrt(step_squares / (HEAD_COUNT * HDIM) + EPSILON)
    decode_out = (decoded * step_scale[:, :, None] * norm_gain[None, None, :]).astype(jnp.bfloat16)
    return (attn_out, decode_out)


def solution(mesh):
    in_specs = (
        P("seq", "head"),
        P("seq", "head"),
        P("seq", "head"),
        P("seq", "head"),
        P("head"),
        P(),
        P(None, "seq", "head"),
        P(None, "seq", "head"),
        P(None, "seq", "head"),
        P(None, "seq", "head"),
        P("seq"),
    )
    out_specs = (P("seq", "head"), P(None, "seq", "head"))
    return jax.shard_map(local, mesh=mesh, in_specs=in_specs, out_specs=out_specs, check_vma=False)
```

profile of v0, /device:TPU:0, one launch (start us, length us, event | category | flops | bytes accessed | tf_op | source)
XLA Modules:
  0.0 465.3 jit_solution(464305001508278530)
XLA Ops:
  7.2 0.8 copy_bitcast_fusion
  8.8 0.8 reduce-window.10
  13.3 1.5 copy.146
  14.8 2.6 convolution_add_fusion.1
  17.6 1.5 copy.133
  19.1 1.4 copy.135
  20.5 22.7 %all-gather = f32[8,1,16]{2,1,0:T(1,128)S(1)} all-gather(f32[1,1,16]{2,1,0:T(1,128)S(1)} %get-tuple-element.344), channel_id=2, replica_groups=mesh['seq'=8,'head'=4] {'seq'}, dimensions={0}, use_global_device_ids=true | all-gather | bytes 576 | tf_op jit(solution)/shard_map/all_gather | solution.py:15
  43.2 101.7 %all-gather.4.cloned.1.call-done = f32[128,128,128]{2,1,0:T(8,128)} async-done(((f32[16,128,128]{2,1,0:T(8,128)}), f32[128,128,128]{2,1,0:T(8,128)}) %all-gather.4.cloned.1.call-update) | async-done | bytes 8388624 | tf_op jit(solution)/shard_map/all_gather | solution.py:15
  145.0 32.4 %while.26 = (s32[]{:T(128)}, f32[4,16,128,128]{3,2,1,0:T(8,128)}, s32[4]{0:T(128)S(1)}, s32[4]{0:T(128)S(1)}, s32[]{:T(128)}, /*index=5*/f32[1,256,16]{1,2,0:T(8...) while((s32[]{:T(128)}, f32[4,16,128,128]{3,2,1,0:T(8,128)}, ...), condition=%wide.region_10.11_spmd, body=%wide.region_9.10_spmd.sunk | while | flops 136590384 | bytes 4248923 | solution.py:128
  149.0 0.7 compare_reduce_fusion.2
  150.4 2.7 fusion.78
  157.2 0.7 compare_reduce_fusion.2
  158.6 2.6 fusion.78
  165.2 0.7 compare_reduce_fusion.2
  166.7 2.7 fusion.78
  173.3 0.7 compare_reduce_fusion.2
  174.7 2.6 fusion.78
  177.4 1.6 convert_bitcast_fusion.1
  179.7 1.7 convert_bitcast_fusion
  182.1 0.7 copy.153
  182.7 0.7 copy.154
  183.4 1.6 fusion.54
  185.0 1.6 reshape.536
  186.6 1.6 reshape.534
  188.2 1.6 copy.155
  189.8 1.6 copy.156
  191.4 1.6 reshape.538
  193.0 0.7 copy.157
  193.7 1.6 copy.158
  195.2 0.8 reshape.540
  196.8 1.4 exponential_bitcast_fusion
  198.2 4.4 fusion.36
  202.6 4.1 multiply_reduce_fusion
  206.7 1.9 copy.131
  208.7 133.8 %all-reduce.3.cloned.1.call-done = f32[4,16,128,128]{3,2,1,0:T(8,128)} async-done(((f32[4,16,128,128]{3,2,1,0:T(8,128)}), f32[4,16,128,128]{3,2,1,0:T(8,128)}) %all-reduce.3.cloned.1.call-update) | async-done | bytes 4194320 | tf_op jit(solution)/shard_map/psum | solution.py:129
  342.5 10.0 %gather_fusion = f32[16,16,128,128]{3,2,1,0:T(8,128)} fusion(f32[4,16,128,128]{3,2,1,0:T(8,128)} %all-reduce.3.cloned.1.call-done, s32[1024]{0:T(1024)S(1)} %pad_clamp_fusion), kind=kCustom, calls=%fused_computation | custom fusion | bytes 33554496 | tf_op jit(solution)/shard_map/jit(_take)/gather | solution.py:131
  352.5 17.9 %fusion.15 = f32[16,16,1,128]{3,2,1,0:T(1,128)} fusion(bf16[16,16,128,1]{2,3,1,0:T(2,128)(2,1)S(1)} %copy-done.3, f32[16,16,128]{2,1,0:T(8,128)} %bitcast.215, f32[16,16,128]{2,1,0:T(8,128)} %bitcast.212, f32[16,16]{1,0:T(8,128)S(1)} %get-tuple-element.346, f32[16,16,128,128]{3,2,1,0:T(8,128)} %gather_fusion, f32[16,16,128]{2,1,0:T(8,128)} %bitcast.208, ...), kind=kOutput, calls=%fused_computation.28 | convolution fusion | flops 79691776 | bytes 17500176 | tf_op jit(solution)/shard_map/rhd,rhde->rhe/dot_general | solution.py:142
  370.4 0.9 stack_reshape.13
  371.4 13.4 %fusion.52 = f32[16,16,1,128]{3,2,1,0:T(1,128)} fusion(bf16[16,16,128,1]{2,3,1,0:T(2,128)(2,1)S(1)} %copy-done.2, f32[16,16,128,128]{3,2,1,0:T(8,128)} %gather_fusion, f32[16,16,128]{2,1,0:T(8,128)} %bitcast.209, f32[16,16,128]{2,1,0:T(8,128)S(1)} %bitcast.207, f32[16,16]{1,0:T(8,128)} %get-tuple-element.347, pred[16]{0:T(512)(128)(4,1)} %compare_and_fusion.1), kind=kOutput, calls=%fused_computation.108 | convolution fusion | flops 67108864 | bytes 17237008 | tf_op jit(solution)/shard_map/rhd,rhde->rhe/dot_general | solution.py:142
  384.8 0.9 stack_reshape.12
  386.4 22.6 %fusion.16 = f32[16,16,1,128]{3,2,1,0:T(1,128)} fusion(bf16[16,16,128,1]{2,3,1,0:T(2,128)(2,1)} %reshape.538, f32[16,16,128]{2,1,0:T(8,128)} %bitcast.220, f32[16,16,128]{2,1,0:T(8,128)} %bitcast.218, f32[16,16]{1,0:T(8,128)} %get-tuple-element.348, f32[16,16,128]{2,1,0:T(8,128)} %bitcast.216, f32[16,16,128]{2,1,0:T(8,128)} %bitcast.213, ...), kind=kOutput, calls=%fused_computation.29 | convolution fusion | flops 92274688 | bytes 17763344 | tf_op jit(solution)/shard_map/rhd,rhde->rhe/dot_general | solution.py:142
  409.0 0.9 stack_reshape.14
  409.9 34.9 %fusion.11 = f32[16,16,1,128]{3,2,1,0:T(1,128)} fusion(bf16[16,16,128,1]{2,3,1,0:T(2,128)(2,1)S(1)} %copy-done.1, f32[16,16,128]{2,1,0:T(8,128)} %bitcast.223, f32[16,16,128]{2,1,0:T(8,128)} %bitcast.222, f32[16,16]{1,0:T(8,128)S(1)} %get-tuple-element.345, f32[16,16,128]{2,1,0:T(8,128)} %bitcast.221, f32[16,16,128]{2,1,0:T(8,128)} %bitcast.219, ...), kind=kOutput, calls=%fused_computation.21 | convolution fusion | flops 104857600 | bytes 18026512 | tf_op jit(solution)/shard_map/rhd,rhde->rhe/dot_general | solution.py:142
  444.8 0.9 stack_reshape.15
  447.8 1.2 multiply_reduce_fusion.1
  448.9 6.4 %all-reduce = (f32[256]{0:T(256)S(1)}, f32[4,16]{1,0:T(4,128)S(1)}) all-reduce(f32[256]{0:T(256)} %get-tuple-element.351, f32[4,16]{1,0:T(4,128)S(1)} %multiply_reduce_fusion.1), channel_id=1, replica_groups=mesh['seq'=8,'head'=4] {'head'}, use_global_device_ids=true, to_apply=%region_8.9 | all-reduce | flops 320 | bytes 2560 | tf_op jit(solution)/shard_map/psum | solution.py:99
  455.4 1.9 multiply_convert_fusion.4
  457.2 1.2 multiply_convert_fusion.1
  (82 shorter events, 14.1 us)
Async XLA Ops:
  7.2 191.1 %copy-start = (bf16[256,2048]{1,0:T(8,128)(2,1)S(1)}, bf16[256,2048]{1,0:T(8,128)(2,1)}, u32[]{:S(2)}) copy-start(bf16[256,2048]{1,0:T(8,128)(2,1)} %param.15) | copy-start | bytes 3145732
  7.2 137.7 %all-gather.4.cloned.1.call-start = ((), (), s32[]{:S(2)}) async-start(), calls=%async_computation.1 | async-start | bytes 9437184 | tf_op jit(solution)/shard_map/all_gather | solution.py:15
  17.5 325.0 %all-reduce.3.cloned.1.call-start = ((), (), s32[]{:S(2)}) async-start(), calls=%async_computation | async-start | bytes 8388608 | tf_op jit(solution)/shard_map/psum | solution.py:129
  145.0 51.2 %copy-start.7 = (s32[16]{0:T(128)S(1)}, s32[16]{0:T(128)}, u32[]{:S(2)}) copy-start(s32[16]{0:T(128)} %param.25) | copy-start | bytes 196
  198.1 188.2 %copy-start.6 = (f32[16,16]{1,0:T(8,128)}, f32[16,16]{1,0:T(8,128)S(1)}, u32[]{:S(2)}) copy-start(f32[16,16]{1,0:T(8,128)S(1)} %get-tuple-element.346) | copy-start | bytes 3076
  208.6 143.9 %copy-start.3 = (bf16[16,16,128,1]{2,3,1,0:T(2,128)(2,1)S(1)}, bf16[16,16,128,1]{2,3,1,0:T(2,128)(2,1)}, u32[]{:S(2)}) copy-start(bf16[16,16,128,1]{2,3,1,0:T(2,128)(2,1)} %reshape.536) | copy-start | bytes 196612
  208.7 143.8 %copy-start.4 = (f32[2,8,16,128]{3,2,1,0:T(8,128)S(1)}, f32[2,8,16,128]{3,2,1,0:T(8,128)}, u32[]{:S(2)}) copy-start(f32[2,8,16,128]{3,2,1,0:T(8,128)} %copy.151) | copy-start | bytes 393220
  352.5 18.9 %copy-start.2 = (bf16[16,16,128,1]{2,3,1,0:T(2,128)(2,1)S(1)}, bf16[16,16,128,1]{2,3,1,0:T(2,128)(2,1)}, u32[]{:S(2)}) copy-start(bf16[16,16,128,1]{2,3,1,0:T(2,128)(2,1)} %reshape.534) | copy-start | bytes 196612
  386.4 23.6 %copy-start.1 = (bf16[16,16,128,1]{2,3,1,0:T(2,128)(2,1)S(1)}, bf16[16,16,128,1]{2,3,1,0:T(2,128)(2,1)}, u32[]{:S(2)}) copy-start(bf16[16,16,128,1]{2,3,1,0:T(2,128)(2,1)} %reshape.540) | copy-start | bytes 196612
  409.9 45.4 %copy-start.5 = (f32[2048]{0:T(1024)S(1)}, f32[2048]{0:T(1024)}, u32[]{:S(2)}) copy-start(f32[2048]{0:T(1024)} %param.19) | copy-start | bytes 24580
Sparse Core Ops, SparseCore 0:
  17.6 127.2 all-gather.3
  177.5 164.8 all-reduce.2
where the time goes:
time: 467 us; the launch traced here: 465 us
  waiting for transfers between devices  235 us (50%)
  matrix products  111 us (24%)
  local copies, waits for them, and re-layouts  46.8 us (10%)
  blocking collectives  29.1 us (6%)
  between operations  15.6 us (3%)
  other arithmetic  14.4 us (3%)
  loops' own time  13.2 us (3%)
    psum x1, waiting for transfers between devices, local(): prompt_state = lax.psum(candidates, 'seq')  134 us
    all_gather x1, waiting for transfers between devices, carried_in(): gathered = jax.tree.map(lambda a: lax.all_gather(a, axis), part)  102 us
    dot_general x4, matrix products, local(): jnp.einsum('rhd,rhde->rhe', query_now, row_states, precision=lax.Precisio...  88.8 us
    all_gather x1, blocking collectives, carried_in(): gathered = jax.tree.map(lambda a: lax.all_gather(a, axis), part)  22.7 us
    another operation x1, loops' own time, local(): candidates = lax.map(prompt_end, jnp.arange(PROMPTS, dtype=jnp.int32))  13.2 us
    unnamed x28, local copies, waits for them, and re-layouts  11.6 us
    dot_general x4, matrix products, prompt_end(): jnp.einsum('shd,she->hde', tailed, values_blk[blk_index], preferred_eleme...  10.7 us
    gather x1, local copies, waits for them, and re-layouts, local(): row_states = jnp.take(prompt_state, row_prompt, axis=0)  10 us
  transfers between devices with their start and end apart: 2, of which 2 were waited for; matrix products, arithmetic and copies ran while one was open for 7% of the time, Pallas kernels for 0%

commit v1 on v0

--- a/solution.py
+++ b/solution.py
@@ -126,7 +126,11 @@
         return total * owned.astype(jnp.float32)
 
     candidates = lax.map(prompt_end, jnp.arange(PROMPTS, dtype=jnp.int32))
-    prompt_state = lax.psum(candidates, "seq")
+    prompt_state = candidates
+    for hop in (1, 2, 4):
+        prompt_state = prompt_state + lax.ppermute(
+            prompt_state, "seq", [(dev, dev ^ hop) for dev in range(8)]
+        )
     rows_here = row_prompt.shape[0]
     row_states = jnp.take(prompt_state, row_prompt, axis=0)
     results = []

time: 467 us -> 682 us (1.46)
  waiting for transfers between devices: 235 us -> 439 us
  starting transfers between devices: 0.08 us -> 14.5 us
  other arithmetic: 14.4 us -> 22.2 us
  local copies, waits for them, and re-layouts: 46.8 us -> 39.5 us
    ppermute x0 -> x3, waiting for transfers between devices: none -> 337 us  [local(): lax.ppermute(prompt_state, 'seq', [(dev, dev ^ hop) for dev in range(8)])]
    psum x1 -> x0, waiting for transfers between devices: 134 us -> none  [local(): prompt_state = lax.psum(candidates, 'seq')]
    ppermute x0 -> x3, starting transfers between devices: none -> 14.5 us  [local(): lax.ppermute(prompt_state, 'seq', [(dev, dev ^ hop) for dev in range(8)])]
    add x0 -> x3, other arithmetic: none -> 12.1 us  [local(): prompt_state + lax.ppermute(prompt_state, 'seq', [(dev, dev ^ hop) for de...]
  transfers between devices with their start and end apart: 2 -> 4, of which waited for: 2 -> 4; matrix products, arithmetic and copies ran while one was open for 7% -> 4% of each run, Pallas kernels for 0% -> 0%
where the time goes in v1:
time: 682 us; the launch traced here: 681 us
  waiting for transfers between devices  439 us (64%)
  matrix products  109 us (16%)
  local copies, waits for them, and re-layouts  39.5 us (6%)
  blocking collectives  28.6 us (4%)
  other arithmetic  22.2 us (3%)
  between operations  15.7 us (2%)
  starting transfers between devices  14.5 us (2%)
  loops' own time  13.2 us (2%)
    ppermute x3, waiting for transfers between devices, local(): lax.ppermute(prompt_state, 'seq', [(dev, dev ^ hop) for dev in range(8)])  337 us
    all_gather x1, waiting for transfers between devices, carried_in(): gathered = jax.tree.map(lambda a: lax.all_gather(a, axis), part)  102 us
    dot_general x4, matrix products, local(): jnp.einsum('rhd,rhde->rhe', query_now, row_states, precision=lax.Precisio...  87 us
    all_gather x1, blocking collectives, carried_in(): gathered = jax.tree.map(lambda a: lax.all_gather(a, axis), part)  22.7 us
    ppermute x3, starting transfers between devices, local(): lax.ppermute(prompt_state, 'seq', [(dev, dev ^ hop) for dev in range(8)])  14.5 us
  transfers between devices with their start and end apart: 4, of which 4 were waited for; matrix products, arithmetic and copies ran while one was open for 4% of the time, Pallas kernels for 0%

profile of v1, /device:TPU:0, one launch (start us, length us, event | category | flops | bytes accessed | tf_op | source)
XLA Modules:
  0.0 680.9 jit_solution(9765093756036271642)
XLA Ops:
  7.2 0.8 copy_bitcast_fusion
  8.8 0.8 reduce-window.10
  13.3 1.5 copy.146
  14.8 2.6 convolution_add_fusion.1
  17.6 1.5 copy.133
  19.1 1.3 copy.135
  20.4 22.7 %all-gather = f32[8,1,16]{2,1,0:T(1,128)S(1)} all-gather(f32[1,1,16]{2,1,0:T(1,128)S(1)} %get-tuple-element.344), channel_id=2, replica_groups=mesh['seq'=8,'head'=4] {'seq'}, dimensions={0}, use_global_device_ids=true | all-gather | bytes 576 | tf_op jit(solution)/shard_map/all_gather | solution.py:15
  43.1 101.7 %all-gather.4.cloned.1.call-done = f32[128,128,128]{2,1,0:T(8,128)} async-done(((f32[16,128,128]{2,1,0:T(8,128)}), f32[128,128,128]{2,1,0:T(8,128)}) %all-gather.4.cloned.1.call-update) | async-done | bytes 8388624 | tf_op jit(solution)/shard_map/all_gather | solution.py:15
  145.0 32.3 %while.26 = (s32[]{:T(128)}, f32[4,16,128,128]{3,2,1,0:T(8,128)}, s32[4]{0:T(128)S(1)}, s32[4]{0:T(128)S(1)}, s32[]{:T(128)}, /*index=5*/f32[1,256,16]{1,2,0:T(8...) while((s32[]{:T(128)}, f32[4,16,128,128]{3,2,1,0:T(8,128)}, ...), condition=%wide.region_10.11_spmd, body=%wide.region_9.10_spmd.sunk | while | flops 136590384 | bytes 4248923 | solution.py:128
  150.4 2.7 fusion.78
  158.6 2.6 fusion.78
  166.6 2.7 fusion.78
  174.7 2.7 fusion.78
  177.4 2.1 collective-permute-start
  179.5 90.1 %collective-permute-done = f32[4,16,128,128]{3,2,1,0:T(8,128)S(1)} collective-permute-done((f32[4,16,128,128]{3,2,1,0:T(8,128)}, f32[4,16,128,128]{3,2,1,0:T(8,128)S(1)}, u32[]{:S(2)}, u32[]{:S(2)}) %collective-permute-start) | collective-permute-done | bytes 4194336 | tf_op jit(solution)/shard_map/ppermute | solution.py:131
  269.5 2.9 add.130
  272.5 2.9 collective-permute-start.1
  275.4 89.5 %collective-permute-done.1 = f32[4,16,128,128]{3,2,1,0:T(8,128)S(1)} collective-permute-done((f32[4,16,128,128]{3,2,1,0:T(8,128)S(1)}, f32[4,16,128,128]{3,2,1,0:T(8,128)S(1)}, u32[]{:S(2)}, u32[]{:S(2)}) %collective-permute-start.1) | collective-permute-done | bytes 4194336 | tf_op jit(solution)/shard_map/ppermute | solution.py:131
  364.9 2.7 add.131
  367.6 9.5 %collective-permute-start.2 = (f32[4,16,128,128]{3,2,1,0:T(8,128)}, f32[4,16,128,128]{3,2,1,0:T(8,128)}, u32[]{:S(2)}, u32[]{:S(2)}) collective-permute-start(f32[4,16,128,128]{3,2,1,0:T(8,128)} %add.131), channel_id=1, source_target_pairs={{0,16},{4,20},{8,24},{12,28},{16,0},{20,4},{24,8},{28,12},{1,17},{... | collective-permute-start | bytes 12582920 | tf_op jit(solution)/shard_map/ppermute | solution.py:131
  377.8 0.7 copy.152
  378.5 0.7 copy.153
  379.2 0.7 copy.154
  379.9 0.7 copy.155
  380.6 0.7 copy.156
  381.9 0.7 copy.158
  383.3 1.6 reshape.540
  384.9 0.7 reshape.538
  385.6 0.7 reshape.536
  386.3 0.7 reshape.534
  387.8 1.3 exponential_bitcast_fusion
  389.3 4.3 fusion.36
  393.6 4.0 multiply_reduce_fusion
  397.6 1.9 copy.131
  399.5 157.3 %collective-permute-done.2 = f32[4,16,128,128]{3,2,1,0:T(8,128)} collective-permute-done((f32[4,16,128,128]{3,2,1,0:T(8,128)}, f32[4,16,128,128]{3,2,1,0:T(8,128)}, u32[]{:S(2)}, u32[]{:S(2)}) %collective-permute-start.2) | collective-permute-done | bytes 4194336 | tf_op jit(solution)/shard_map/ppermute | solution.py:131
  556.8 6.5 add.132
  563.3 10.1 %gather_fusion = f32[16,16,128,128]{3,2,1,0:T(8,128)} fusion(f32[4,16,128,128]{3,2,1,0:T(8,128)} %add.132, s32[1024]{0:T(1024)S(1)} %pad_clamp_fusion), kind=kCustom, calls=%fused_computation | custom fusion | bytes 33554496 | tf_op jit(solution)/shard_map/jit(_take)/gather | solution.py:135
  573.6 32.5 %fusion.11 = f32[16,16,1,128]{3,2,1,0:T(1,128)S(1)} fusion(bf16[16,16,128,1]{2,3,1,0:T(2,128)(2,1)S(1)} %copy-done.8, f32[16,16,128]{2,1,0:T(8,128)S(1)} %bitcast.223, f32[16,16,128]{2,1,0:T(8,128)S(1)} %bitcast.222, f32[16,16]{1,0:T(8,128)} %get-tuple-element.345, f32[16,16,128]{2,1,0:T(8,128)S(1)} %bitcast.220, f32[16,16,128]{2,1,0:T(8,128)S(1)} %bitcast.218, ...), kind=kOutput, calls=%fused_computation.21 | convolution fusion | flops 104857600 | bytes 18026512 | tf_op jit(solution)/shard_map/rhd,rhde->rhe/dot_general | solution.py:146
  606.1 23.1 %fusion.16 = f32[16,16,1,128]{3,2,1,0:T(1,128)S(1)} fusion(bf16[16,16,128,1]{2,3,1,0:T(2,128)(2,1)S(1)} %copy-done.7, f32[16,16,128]{2,1,0:T(8,128)S(1)} %bitcast.221, f32[16,16,128]{2,1,0:T(8,128)S(1)} %bitcast.219, f32[16,16]{1,0:T(8,128)} %get-tuple-element.348, f32[16,16,128]{2,1,0:T(8,128)S(1)} %bitcast.217, f32[16,16,128]{2,1,0:T(8,128)S(1)} %bitcast.214, ...), kind=kOutput, calls=%fused_computation.29 | convolution fusion | flops 92274688 | bytes 17763344 | tf_op jit(solution)/shard_map/rhd,rhde->rhe/dot_general | solution.py:146
  629.2 18.0 %fusion.15 = f32[16,16,1,128]{3,2,1,0:T(1,128)} fusion(bf16[16,16,128,1]{2,3,1,0:T(2,128)(2,1)S(1)} %copy-done.6, f32[16,16,128]{2,1,0:T(8,128)} %bitcast.215, f32[16,16,128]{2,1,0:T(8,128)} %bitcast.212, f32[16,16]{1,0:T(8,128)S(1)} %get-tuple-element.346, f32[16,16,128,128]{3,2,1,0:T(8,128)} %gather_fusion, f32[16,16,128]{2,1,0:T(8,128)} %bitcast.208, ...), kind=kOutput, calls=%fused_computation.28 | convolution fusion | flops 79691776 | bytes 17500176 | tf_op jit(solution)/shard_map/rhd,rhde->rhe/dot_general | solution.py:146
  647.3 0.9 stack_reshape.13
  648.2 13.4 %fusion.52 = f32[16,16,1,128]{3,2,1,0:T(1,128)} fusion(bf16[16,16,128,1]{2,3,1,0:T(2,128)(2,1)} %reshape.534, f32[16,16,128,128]{3,2,1,0:T(8,128)} %gather_fusion, f32[16,16,128]{2,1,0:T(8,128)} %bitcast.209, f32[16,16,128]{2,1,0:T(8,128)} %bitcast.205, f32[16,16]{1,0:T(8,128)S(1)} %get-tuple-element.347, pred[16]{0:T(512)(128)(4,1)} %compare_and_fusion.1), kind=kOutput, calls=%fused_computation.108 | convolution fusion | flops 67108864 | bytes 17237008 | tf_op jit(solution)/shard_map/rhd,rhde->rhe/dot_general | solution.py:146
  661.6 1.6 stack_reshape.12
  663.2 0.9 constant_dynamic-update-slice_fusion.3
  664.2 0.8 copy-done.2
  665.1 5.8 all-reduce
  671.0 1.9 multiply_convert_fusion.4
  672.8 1.2 multiply_convert_fusion.1
  (110 shorter events, 15.0 us)
Async XLA Ops:
  7.2 382.1 %copy-start = (bf16[256,2048]{1,0:T(8,128)(2,1)S(1)}, bf16[256,2048]{1,0:T(8,128)(2,1)}, u32[]{:S(2)}) copy-start(bf16[256,2048]{1,0:T(8,128)(2,1)} %param.15) | copy-start | bytes 3145732
  7.2 137.7 %all-gather.4.cloned.1.call-start = ((), (), s32[]{:S(2)}) async-start(), calls=%async_computation | async-start | bytes 9437184 | tf_op jit(solution)/shard_map/all_gather | solution.py:15
  177.3 199.7 %copy-start.3 = (bf16[4,16,2048]{2,1,0:T(8,128)(2,1)S(1)}, bf16[4,16,2048]{2,1,0:T(8,128)(2,1)}, u32[]{:S(2)}) copy-start(bf16[4,16,2048]{2,1,0:T(8,128)(2,1)} %param.22) | copy-start | bytes 786436
  177.3 200.5 %copy-start.4 = (bf16[4,16,2048]{2,1,0:T(8,128)(2,1)S(1)}, bf16[4,16,2048]{2,1,0:T(8,128)(2,1)}, u32[]{:S(2)}) copy-start(bf16[4,16,2048]{2,1,0:T(8,128)(2,1)} %param.23) | copy-start | bytes 786436
  177.3 205.3 %copy-start.5 = (bf16[4,16,2048]{2,1,0:T(8,128)(2,1)S(1)}, bf16[4,16,2048]{2,1,0:T(8,128)(2,1)}, u32[]{:S(2)}) copy-start(bf16[4,16,2048]{2,1,0:T(8,128)(2,1)} %param.21) | copy-start | bytes 786436
  177.4 209.9 %copy-start.18 = (s32[16]{0:T(128)S(1)}, s32[16]{0:T(128)}, u32[]{:S(2)}) copy-start(s32[16]{0:T(128)} %param.25) | copy-start | bytes 196
  177.4 92.2 %collective-permute-start = (f32[4,16,128,128]{3,2,1,0:T(8,128)}, f32[4,16,128,128]{3,2,1,0:T(8,128)S(1)}, u32[]{:S(2)}, u32[]{:S(2)}) collective-permute-start(f32[4,16,128,128]{3,2,1,0:T(8,128)} %get-tuple-element.215), channel_id=1, source_target_pairs={{0,4},{4,0},{8,12},{12,8},{16,20},{20,16},{24,28},{28,24},{1,5},{5... | collective-permute-start | bytes 12582920 | tf_op jit(solution)/shard_map/ppermute | solution.py:131
  272.5 92.4 %collective-permute-start.1 = (f32[4,16,128,128]{3,2,1,0:T(8,128)S(1)}, f32[4,16,128,128]{3,2,1,0:T(8,128)S(1)}, u32[]{:S(2)}, u32[]{:S(2)}) collective-permute-start(f32[4,16,128,128]{3,2,1,0:T(8,128)S(1)} %add.130), channel_id=1, source_target_pairs={{0,8},{4,12},{8,0},{12,4},{16,24},{20,28},{24,16},{28,20},{1,9},{5... | collective-permute-start | bytes 12582920 | tf_op jit(solution)/shard_map/ppermute | solution.py:131
  367.6 189.2 %collective-permute-start.2 = (f32[4,16,128,128]{3,2,1,0:T(8,128)}, f32[4,16,128,128]{3,2,1,0:T(8,128)}, u32[]{:S(2)}, u32[]{:S(2)}) collective-permute-start(f32[4,16,128,128]{3,2,1,0:T(8,128)} %add.131), channel_id=1, source_target_pairs={{0,16},{4,20},{8,24},{12,28},{16,0},{20,4},{24,8},{28,12},{1,17},{... | collective-permute-start | bytes 12582920 | tf_op jit(solution)/shard_map/ppermute | solution.py:131
  563.3 10.2 %copy-start.8 = (bf16[16,16,128,1]{2,3,1,0:T(2,128)(2,1)S(1)}, bf16[16,16,128,1]{2,3,1,0:T(2,128)(2,1)}, u32[]{:S(2)}) copy-start(bf16[16,16,128,1]{2,3,1,0:T(2,128)(2,1)} %reshape.540) | copy-start | bytes 196612
  563.3 10.2 %copy-start.9 = (f32[2,8,16,128]{3,2,1,0:T(8,128)S(1)}, f32[2,8,16,128]{3,2,1,0:T(8,128)}, u32[]{:S(2)}) copy-start(f32[2,8,16,128]{3,2,1,0:T(8,128)} %copy.151) | copy-start | bytes 393220
  563.3 10.2 %copy-start.10 = (f32[2,8,16,128]{3,2,1,0:T(8,128)S(1)}, f32[2,8,16,128]{3,2,1,0:T(8,128)}, u32[]{:S(2)}) copy-start(f32[2,8,16,128]{3,2,1,0:T(8,128)} %copy.152) | copy-start | bytes 393220
  563.3 10.2 %copy-start.11 = (f32[2,8,16,128]{3,2,1,0:T(8,128)S(1)}, f32[2,8,16,128]{3,2,1,0:T(8,128)}, u32[]{:S(2)}) copy-start(f32[2,8,16,128]{3,2,1,0:T(8,128)} %copy.153) | copy-start | bytes 393220
  563.3 10.2 %copy-start.12 = (f32[2,8,16,128]{3,2,1,0:T(8,128)S(1)}, f32[2,8,16,128]{3,2,1,0:T(8,128)}, u32[]{:S(2)}) copy-start(f32[2,8,16,128]{3,2,1,0:T(8,128)} %copy.154) | copy-start | bytes 393220
  563.3 10.2 %copy-start.13 = (f32[2,8,16,128]{3,2,1,0:T(8,128)S(1)}, f32[2,8,16,128]{3,2,1,0:T(8,128)}, u32[]{:S(2)}) copy-start(f32[2,8,16,128]{3,2,1,0:T(8,128)} %copy.155) | copy-start | bytes 393220
  563.3 10.2 %copy-start.14 = (f32[2,8,16,128]{3,2,1,0:T(8,128)S(1)}, f32[2,8,16,128]{3,2,1,0:T(8,128)}, u32[]{:S(2)}) copy-start(f32[2,8,16,128]{3,2,1,0:T(8,128)} %copy.156) | copy-start | bytes 393220
  563.3 10.2 %copy-start.15 = (f32[2,8,16,128]{3,2,1,0:T(8,128)S(1)}, f32[2,8,16,128]{3,2,1,0:T(8,128)}, u32[]{:S(2)}) copy-start(f32[2,8,16,128]{3,2,1,0:T(8,128)} %copy.157) | copy-start | bytes 393220
  563.3 10.2 %copy-start.16 = (f32[2,8,16,128]{3,2,1,0:T(8,128)S(1)}, f32[2,8,16,128]{3,2,1,0:T(8,128)}, u32[]{:S(2)}) copy-start(f32[2,8,16,128]{3,2,1,0:T(8,128)} %copy.158) | copy-start | bytes 393220
  573.6 32.5 %copy-start.7 = (bf16[16,16,128,1]{2,3,1,0:T(2,128)(2,1)S(1)}, bf16[16,16,128,1]{2,3,1,0:T(2,128)(2,1)}, u32[]{:S(2)}) copy-start(bf16[16,16,128,1]{2,3,1,0:T(2,128)(2,1)} %reshape.538) | copy-start | bytes 196612
  606.1 23.1 %copy-start.6 = (bf16[16,16,128,1]{2,3,1,0:T(2,128)(2,1)S(1)}, bf16[16,16,128,1]{2,3,1,0:T(2,128)(2,1)}, u32[]{:S(2)}) copy-start(bf16[16,16,128,1]{2,3,1,0:T(2,128)(2,1)} %reshape.536) | copy-start | bytes 196612
  629.2 44.8 %copy-start.1 = (bf16[256,2048]{1,0:T(8,128)(2,1)S(1)}, bf16[256,2048]{1,0:T(8,128)(2,1)}, u32[]{:S(2)}) copy-start(bf16[256,2048]{1,0:T(8,128)(2,1)} %param.15) | copy-start | bytes 3145732
  647.3 23.7 %copy-start.17 = (f32[2048]{0:T(1024)S(1)}, f32[2048]{0:T(1024)}, u32[]{:S(2)}) copy-start(f32[2048]{0:T(1024)} %param.19) | copy-start | bytes 24580
  664.2 0.8 copy-start.2
Sparse Core Ops, SparseCore 0:
  17.6 127.2 all-gather.3
